TPU v7x, 32 devices: a whole 2x2x4 slice. The times are simulated.
32 devices in a mesh: dp: 2 (over core), tensor: 16 (over z, y, x).
Axes of the slice: x: 2, y: 2, z: 4, core: 2. Of those that a mesh axis runs over, the one named last changes fastest.
Arguments:
- gradient: float32 [2, 8192, 512], P('dp', 'tensor'), may hold values from -80 to 80
Outputs:
- update: bfloat16 [2, 8192, 512], P(None, 'tensor')
All inputs are finite; a program needn't handle non-finite values.
Results may differ from a plain program's by a relative error of at most 0.001.
Values may be sent and summed in bfloat16 or wider, within the bound.
No kernel may reach another device: no remote copies, remote signals or barrier semaphores. Data moves between devices by JAX's collectives and lax.ppermute only.
A program may use at most 64 MiB of HBM per device.

v0:
```python
import math

import jax
import jax.numpy as jnp
from jax import lax
from jax.sharding import PartitionSpec as P

FEATURES = 8192
OUTPUTS = 512
ITERS = 3


linear_term = 3.4445
cubic_term = -4.775
quintic_term = 2.0315
norm_floor = 1e-07
update_gain = 0.2


def multiply(first_factor, second_factor):
    return jnp.einsum("mrs,mst->mrt", first_factor, second_factor, precision=lax.Precision.HIGHEST)


def local_gram(gradient):
    return jnp.einsum("mfr,mfs->mrs", gradient, gradient, precision=lax.Precision.HIGHEST)


def reduce_gram(partial_gram):
    return lax.psum(partial_gram, "tensor")


def replicated_total(gram_matrix):
    order = gram_matrix.shape[2]
    identity = jnp.eye(order, dtype=jnp.float32)[None]
    running = identity
    for turn_index in range(ITERS):
        squared = multiply(gram_matrix, gram_matrix)
        polynomial = linear_term * identity + cubic_term * gram_matrix + quintic_term * squared
        if turn_index == 0:
            running = polynomial
        else:
            running = multiply(running, polynomial)
        if turn_index + 1 < ITERS:
            gram_matrix = multiply(multiply(polynomial, gram_matrix), polynomial)
    return running


def on_device(gradient):
    summed = reduce_gram(local_gram(gradient))
    squared_norm = lax.psum(jnp.sum(gradient * gradient, axis=(1, 2)), "tensor")
    divisor = jnp.sqrt(squared_norm) + norm_floor
    gram_matrix = summed / (divisor * divisor)[:, None, None]
    polished = jnp.einsum(
        "mfr,mrs->mfs", gradient, replicated_total(gram_matrix), precision=lax.Precision.HIGHEST
    )
    factor = update_gain * math.sqrt(max(FEATURES, OUTPUTS)) / divisor
    update = (factor[:, None, None] * polished).astype(jnp.bfloat16)
    return lax.all_gather(update, "dp", axis=0, tiled=True)


def solution(mesh):
    placed = (P("dp", "tensor", None),)
    return jax.shard_map(
        on_device, mesh=mesh, in_specs=placed, out_specs=P(None, "tensor", None), check_vma=False
    )
```

profile of v0, /device:TPU:0, one launch (start us, length us, event | category | flops | bytes accessed | tf_op | source)
XLA Modules:
  0.0 168.9 jit_solution(15192486878711117701)
XLA Ops:
  6.5 0.0 all-reduce.2.cloned.1.call-start
  6.5 4.6 %convolution_bitcast_fusion = f32[1,512,512]{2,1,0:T(8,128)} fusion(f32[1,512,512]{2,1,0:T(8,128)} %param.1), kind=kOutput, calls=%fused_computation.9 | convolution fusion | flops 1610612736 | bytes 2097152 | tf_op jit(solution)/shard_map/mfr,mfs->mrs/dot_general | solution.py:25
  11.2 0.0 copy-start
  11.2 0.0 all-reduce.2.cloned.1.call-update
  11.2 0.0 all-gather.3.cloned.1.call-start
  11.3 1.1 copy-done
  12.4 0.9 multiply_reduce_fusion
  13.3 44.5 %psum.14 = f32[1]{0:T(128)} all-reduce(f32[1]{0:T(128)} %bitcast), channel_id=1, replica_groups=mesh['dp'=2,'tensor'=16] {'tensor'}, use_global_device_ids=true, to_apply=%region_1.0 | all-reduce | flops 1 | bytes 8 | tf_op jit(solution)/shard_map/psum | solution.py:50
  58.5 69.5 %all-reduce.2.cloned.1.call-done = f32[1,512,512]{2,1,0:T(8,128)} async-done(((f32[1,512,512]{2,1,0:T(8,128)}), f32[1,512,512]{2,1,0:T(8,128)}) %all-reduce.2.cloned.1.call-update) | async-done | bytes 1048592 | tf_op jit(solution)/shard_map/psum | solution.py:29
  128.0 0.0 copy-start.1
  128.0 4.1 %fusion.4 = f32[512,512]{1,0:T(8,128)S(1)} fusion(f32[1,512,512]{2,1,0:T(8,128)} %all-reduce.2.cloned.1.call-done, f32[]{:T(128)} %bitcast.4), kind=kOutput, calls=%fused_computation.11 | convolution fusion | flops 1612709888 | bytes 2097156 | tf_op jit(solution)/shard_map/mrs,mst->mrt/dot_general | solution.py:21
  132.1 0.0 copy-done.1
  132.1 1.9 %fusion.7 = f32[512,512]{1,0:T(8,128)S(1)} fusion(f32[512,512]{1,0:T(8,128)S(1)} %fusion.4, f32[1,512,512]{2,1,0:T(8,128)S(1)} %copy-done.1, f32[]{:T(128)} %bitcast.4), kind=kOutput, calls=%fused_computation.14 | convolution fusion | flops 1610874880 | bytes 3145732 | tf_op jit(solution)/shard_map/mrs,mst->mrt/dot_general | solution.py:21
  133.9 1.8 %fusion.12 = f32[512,512]{1,0:T(8,128)S(1)} fusion(f32[512,512]{1,0:T(8,128)S(1)} %fusion.7, f32[512,512]{1,0:T(8,128)S(1)} %fusion.4), kind=kOutput, calls=%fused_computation.23 | convolution fusion | flops 1610612736 | bytes 3145728 | tf_op jit(solution)/shard_map/mrs,mst->mrt/dot_general | solution.py:21
  135.8 1.9 %fusion.1 = f32[512,512]{1,0:T(8,128)S(1)} fusion(f32[512,512]{1,0:T(8,128)S(1)} %fusion.12), kind=kOutput, calls=%fused_computation.6 | convolution fusion | flops 1612185600 | bytes 2097152 | tf_op jit(solution)/shard_map/mrs,mst->mrt/dot_general | solution.py:21
  137.7 1.8 %fusion.14 = f32[512,512]{1,0:T(8,128)S(1)} fusion(f32[512,512]{1,0:T(8,128)S(1)} %fusion.1, f32[512,512]{1,0:T(8,128)S(1)} %fusion.12), kind=kOutput, calls=%fused_computation.25 | convolution fusion | flops 1610612736 | bytes 3145728 | tf_op jit(solution)/shard_map/mrs,mst->mrt/dot_general | solution.py:21
  139.6 1.8 %fusion.13 = f32[512,512]{1,0:T(8,128)S(1)} fusion(f32[512,512]{1,0:T(8,128)S(1)} %fusion.4, f32[512,512]{1,0:T(8,128)S(1)} %fusion.1), kind=kOutput, calls=%fused_computation.24 | convolution fusion | flops 1610612736 | bytes 3145728 | tf_op jit(solution)/shard_map/mrs,mst->mrt/dot_general | solution.py:21
  141.4 2.1 %fusion.15 = f32[512,512]{1,0:T(8,128)S(1)} fusion(f32[512,512]{1,0:T(8,128)S(1)} %fusion.14, f32[512,512]{1,0:T(8,128)S(1)} %fusion.1), kind=kOutput, calls=%fused_computation.26 | convolution fusion | flops 1610612736 | bytes 3145728 | tf_op jit(solution)/shard_map/mrs,mst->mrt/dot_general | solution.py:21
  143.5 1.9 %fusion = f32[512,512]{1,0:T(8,128)S(1)} fusion(f32[512,512]{1,0:T(8,128)S(1)} %fusion.15), kind=kOutput, calls=%fused_computation.4 | convolution fusion | flops 1612185600 | bytes 2097152 | tf_op jit(solution)/shard_map/mrs,mst->mrt/dot_general | solution.py:21
  145.4 1.8 %fusion.16 = f32[512,512]{1,0:T(8,128)S(1)} fusion(f32[512,512]{1,0:T(8,128)S(1)} %fusion.13, f32[512,512]{1,0:T(8,128)S(1)} %fusion), kind=kOutput, calls=%fused_computation.27 | convolution fusion | flops 1610612736 | bytes 3145728 | tf_op jit(solution)/shard_map/mrs,mst->mrt/dot_general | solution.py:21
  147.3 4.3 %fusion.6 = bf16[512,512]{0,1:T(8,128)(2,1)} fusion(f32[512,512]{1,0:T(8,128)S(1)} %fusion.16, f32[1,512,512]{2,1,0:T(8,128)S(1)} %copy-done, f32[]{:T(128)} %bitcast.1), kind=kOutput, calls=%fused_computation.13 | convolution fusion | flops 1611137024 | bytes 2621444 | tf_op jit(solution)/shard_map/mfr,mrs->mfs/dot_general | solution.py:53
  151.5 0.0 all-gather.3.cloned.1.call-update
  151.6 8.3 %all-gather.3.cloned.1.call-done = bf16[1024,512]{0,1:T(8,128)(2,1)} async-done(((bf16[512,512]{0,1:T(8,128)(2,1)}), bf16[1024,512]{0,1:T(8,128)(2,1)}) %all-gather.3.cloned.1.call-update) | async-done | bytes 1048592 | tf_op jit(solution)/shard_map/all_gather | solution.py:58
  159.8 2.3 %copy.3 = bf16[1024,512]{1,0:T(8,128)(2,1)} copy(bf16[1024,512]{0,1:T(8,128)(2,1)} %all-gather.3.cloned.1.call-done) | data formatting | bytes 2097152 | tf_op jit(solution)/shard_map/all_gather | solution.py:58
Async XLA Ops:
  6.5 121.5 %all-reduce.2.cloned.1.call-start = ((), (), s32[]{:S(2)}) async-start(), calls=%async_computation | async-start | bytes 2097152 | tf_op jit(solution)/shard_map/psum | solution.py:29
  11.2 1.2 copy-start
  11.2 148.6 %all-gather.3.cloned.1.call-start = ((), (), s32[]{:S(2)}) async-start(), calls=%async_computation.1 | async-start | bytes 1572864 | tf_op jit(solution)/shard_map/all_gather | solution.py:58
  128.0 4.1 %copy-start.1 = (f32[1,512,512]{2,1,0:T(8,128)S(1)}, f32[1,512,512]{2,1,0:T(8,128)}, u32[]{:S(2)}) copy-start(f32[1,512,512]{2,1,0:T(8,128)} %all-reduce.2.cloned.1.call-done) | copy-start | bytes 3145732
Sparse Core Ops, SparseCore 0:
  12.6 115.3 all-reduce.1
  151.7 8.0 all-gather.2
where the time goes:
time: 169 us
  waiting for transfers between devices  77.8 us (46%)
  blocking collectives  44.5 us (26%)
  matrix products  28.1 us (17%)
  between operations  14.1 us (8%)
  local copies, waits for them, and re-layouts  3.43 us (2%)
    psum x1, waiting for transfers between devices, reduce_gram(): return lax.psum(partial_gram, 'tensor')  69.5 us
    psum x1, blocking collectives, on_device(): squared_norm = lax.psum(jnp.sum(gradient * gradient, axis=(1, 2)), 'tensor')  44.5 us
    dot_general x9, matrix products, multiply(): jnp.einsum('mrs,mst->mrt', first_factor, second_factor, precision=lax.Pre...  19.2 us
    all_gather x1, waiting for transfers between devices, on_device(): return lax.all_gather(update, 'dp', axis=0, tiled=True)  8.26 us
    dot_general x1, matrix products, local_gram(): jnp.einsum('mfr,mfs->mrs', gradient, gradient, precision=lax.Precision.HI...  4.64 us
    dot_general x1, matrix products, on_device(): jnp.einsum('mfr,mrs->mfs', gradient, replicated_total(gram_matrix), preci...  4.28 us
  transfers between devices with their start and end apart: 2, of which 2 were waited for; matrix products, arithmetic and copies ran while one was open for 1% of the time, Pallas kernels for 0%

commit v1 on v0

--- a/solution.py
+++ b/solution.py
@@ -47,7 +47,7 @@
 
 def on_device(gradient):
     summed = reduce_gram(local_gram(gradient))
-    squared_norm = lax.psum(jnp.sum(gradient * gradient, axis=(1, 2)), "tensor")
+    squared_norm = jnp.trace(summed, axis1=1, axis2=2)
     divisor = jnp.sqrt(squared_norm) + norm_floor
     gram_matrix = summed / (divisor * divisor)[:, None, None]
     polished = jnp.einsum(

time: 169 us -> 172 us (1.018)
  waiting for transfers between devices: 77.8 us -> 125 us
  blocking collectives: 44.5 us -> 0 us
  matrix products: 28.1 us -> 26.3 us
    psum x1, waiting for transfers between devices: 69.5 us -> 117 us  [reduce_gram(): return lax.psum(partial_gram, 'tensor')]
    psum x1 -> x0, blocking collectives: 44.5 us -> none  [on_device(): squared_norm = lax.psum(jnp.sum(gradient * gradient, axis=(1, 2)), 'tensor')]
    dot_general x1, matrix products: 4.64 us -> 2.83 us  [local_gram(): jnp.einsum('mfr,mfs->mrs', gradient, gradient, precision=lax.Precision.HI...]
  transfers between devices with their start and end apart: 2 -> 2, of which waited for: 2 -> 2; matrix products, arithmetic and copies ran while one was open for 1% -> 0% of each run, Pallas kernels for 0% -> 0%
where the time goes in v1:
time: 172 us; the launch traced here: 171 us
  waiting for transfers between devices  125 us (73%)
  matrix products  26.3 us (15%)
  between operations  14.2 us (8%)
  local copies, waits for them, and re-layouts  3.5 us (2%)
  other arithmetic  1.99 us (1%)
    psum x1, waiting for transfers between devices, reduce_gram(): return lax.psum(partial_gram, 'tensor')  117 us
    dot_general x9, matrix products, multiply(): jnp.einsum('mrs,mst->mrt', first_factor, second_factor, precision=lax.Pre...  19.2 us
    all_gather x1, waiting for transfers between devices, on_device(): return lax.all_gather(update, 'dp', axis=0, tiled=True)  8.26 us
    dot_general x1, matrix products, on_device(): jnp.einsum('mfr,mrs->mfs', gradient, replicated_total(gram_matrix), preci...  4.28 us
  transfers between devices with their start and end apart: 2, of which 2 were waited for; matrix products, arithmetic and copies ran while one was open for 0% of the time, Pallas kernels for 0%

profile of v1, /device:TPU:0, one launch (start us, length us, event | category | flops | bytes accessed | tf_op | source)
XLA Modules:
  0.0 171.5 jit_solution(2133667007509548431)
XLA Ops:
  6.5 0.0 copy-start
  6.5 0.0 all-reduce.2.cloned.1.call-start
  6.5 1.2 copy-done
  7.8 2.8 %convolution_bitcast_fusion = f32[1,512,512]{2,1,0:T(8,128)} fusion(f32[1,512,512]{2,1,0:T(8,128)S(1)} %copy-done), kind=kOutput, calls=%fused_computation.9 | convolution fusion | flops 1610612736 | bytes 2097152 | tf_op jit(solution)/shard_map/mfr,mfs->mrs/dot_general | solution.py:25
  10.6 0.0 all-reduce.2.cloned.1.call-update
  10.6 0.0 all-gather.3.cloned.1.call-start
  10.7 117.1 %all-reduce.2.cloned.1.call-done = f32[1,512,512]{2,1,0:T(8,128)} async-done(((f32[1,512,512]{2,1,0:T(8,128)}), f32[1,512,512]{2,1,0:T(8,128)}) %all-reduce.2.cloned.1.call-update) | async-done | bytes 1048592 | tf_op jit(solution)/shard_map/psum | solution.py:29
  127.8 0.0 copy-start.1
  127.8 2.0 %select_reduce_fusion = f32[]{:T(128)} fusion(f32[1,512,512]{2,1,0:T(8,128)} %all-reduce.2.cloned.1.call-done), kind=kLoop, calls=%fused_computation.20 | loop fusion | flops 786431 | bytes 1048580 | tf_op jit(solution)/shard_map/jit(trace)/reduce_sum | solution.py:50
  130.5 0.0 copy-done.1
  130.5 1.9 %fusion.4 = f32[512,512]{1,0:T(8,128)S(1)} fusion(f32[1,512,512]{2,1,0:T(8,128)S(1)} %copy-done.1, f32[]{:T(128)S(6)} %mul.52), kind=kOutput, calls=%fused_computation.11 | convolution fusion | flops 1612709888 | bytes 2097156 | tf_op jit(solution)/shard_map/mrs,mst->mrt/dot_general | solution.py:21
  132.5 1.9 %fusion.7 = f32[512,512]{1,0:T(8,128)S(1)} fusion(f32[512,512]{1,0:T(8,128)S(1)} %fusion.4, f32[1,512,512]{2,1,0:T(8,128)S(1)} %copy-done.1, f32[]{:T(128)S(6)} %mul.52), kind=kOutput, calls=%fused_computation.14 | convolution fusion | flops 1610874880 | bytes 3145732 | tf_op jit(solution)/shard_map/mrs,mst->mrt/dot_general | solution.py:21
  134.3 1.8 %fusion.12 = f32[512,512]{1,0:T(8,128)S(1)} fusion(f32[512,512]{1,0:T(8,128)S(1)} %fusion.7, f32[512,512]{1,0:T(8,128)S(1)} %fusion.4), kind=kOutput, calls=%fused_computation.23 | convolution fusion | flops 1610612736 | bytes 3145728 | tf_op jit(solution)/shard_map/mrs,mst->mrt/dot_general | solution.py:21
  136.2 1.9 %fusion.1 = f32[512,512]{1,0:T(8,128)S(1)} fusion(f32[512,512]{1,0:T(8,128)S(1)} %fusion.12), kind=kOutput, calls=%fused_computation.6 | convolution fusion | flops 1612185600 | bytes 2097152 | tf_op jit(solution)/shard_map/mrs,mst->mrt/dot_general | solution.py:21
  138.1 2.8 %fusion.14 = f32[512,512]{1,0:T(8,128)} fusion(f32[512,512]{1,0:T(8,128)S(1)} %fusion.1, f32[512,512]{1,0:T(8,128)S(1)} %fusion.12), kind=kOutput, calls=%fused_computation.25 | convolution fusion | flops 1610612736 | bytes 3145728 | tf_op jit(solution)/shard_map/mrs,mst->mrt/dot_general | solution.py:21
  140.9 1.8 %fusion.13 = f32[512,512]{1,0:T(8,128)S(1)} fusion(f32[512,512]{1,0:T(8,128)S(1)} %fusion.4, f32[512,512]{1,0:T(8,128)S(1)} %fusion.1), kind=kOutput, calls=%fused_computation.24 | convolution fusion | flops 1610612736 | bytes 3145728 | tf_op jit(solution)/shard_map/mrs,mst->mrt/dot_general | solution.py:21
  142.8 3.2 %fusion.15 = f32[512,512]{1,0:T(8,128)S(1)} fusion(f32[512,512]{1,0:T(8,128)} %fusion.14, f32[512,512]{1,0:T(8,128)S(1)} %fusion.1), kind=kOutput, calls=%fused_computation.26 | convolution fusion | flops 1610612736 | bytes 3145728 | tf_op jit(solution)/shard_map/mrs,mst->mrt/dot_general | solution.py:21
  146.1 1.9 %fusion = f32[512,512]{1,0:T(8,128)S(1)} fusion(f32[512,512]{1,0:T(8,128)S(1)} %fusion.15), kind=kOutput, calls=%fused_computation.4 | convolution fusion | flops 1612185600 | bytes 2097152 | tf_op jit(solution)/shard_map/mrs,mst->mrt/dot_general | solution.py:21
  148.0 1.8 %fusion.16 = f32[512,512]{1,0:T(8,128)S(1)} fusion(f32[512,512]{1,0:T(8,128)S(1)} %fusion.13, f32[512,512]{1,0:T(8,128)S(1)} %fusion), kind=kOutput, calls=%fused_computation.27 | convolution fusion | flops 1610612736 | bytes 3145728 | tf_op jit(solution)/shard_map/mrs,mst->mrt/dot_general | solution.py:21
  149.8 4.3 %fusion.6 = bf16[512,512]{0,1:T(8,128)(2,1)} fusion(f32[512,512]{1,0:T(8,128)S(1)} %fusion.16, f32[1,512,512]{2,1,0:T(8,128)S(1)} %copy-done, f32[]{:T(128)S(6)} %div.12), kind=kOutput, calls=%fused_computation.13 | convolution fusion | flops 1611137024 | bytes 2621444 | tf_op jit(solution)/shard_map/mfr,mrs->mfs/dot_general | solution.py:53
  154.1 0.0 all-gather.3.cloned.1.call-update
  154.1 8.3 %all-gather.3.cloned.1.call-done = bf16[1024,512]{0,1:T(8,128)(2,1)} async-done(((bf16[512,512]{0,1:T(8,128)(2,1)}), bf16[1024,512]{0,1:T(8,128)(2,1)}) %all-gather.3.cloned.1.call-update) | async-done | bytes 1048592 | tf_op jit(solution)/shard_map/all_gather | solution.py:58
  162.4 2.3 %copy.3 = bf16[1024,512]{1,0:T(8,128)(2,1)} copy(bf16[1024,512]{0,1:T(8,128)(2,1)} %all-gather.3.cloned.1.call-done) | data formatting | bytes 2097152 | tf_op jit(solution)/shard_map/all_gather | solution.py:58
Async XLA Ops:
  6.5 1.2 copy-start
  6.5 121.3 %all-reduce.2.cloned.1.call-start = ((), (), s32[]{:S(2)}) async-start(), calls=%async_computation | async-start | bytes 2097152 | tf_op jit(solution)/shard_map/psum | solution.py:29
  10.6 151.8 %all-gather.3.cloned.1.call-start = ((), (), s32[]{:S(2)}) async-start(), calls=%async_computation.1 | async-start | bytes 1572864 | tf_op jit(solution)/shard_map/all_gather | solution.py:58
  127.8 2.7 %copy-start.1 = (f32[1,512,512]{2,1,0:T(8,128)S(1)}, f32[1,512,512]{2,1,0:T(8,128)}, u32[]{:S(2)}) copy-start(f32[1,512,512]{2,1,0:T(8,128)} %all-reduce.2.cloned.1.call-done) | copy-start | bytes 3145732
Sparse Core Ops, SparseCore 0:
  12.6 115.1 all-reduce.1
  154.2 8.0 all-gather.2
